TPU v7x, 32 devices: a whole 2x2x4 slice. The times are simulated.
32 devices in a mesh: coil: 4 (over x, core), slab: 8 (over z, y).
Axes of the slice: x: 2, y: 2, z: 4, core: 2. Of those that a mesh axis runs over, the one named last changes fastest.
Arguments:
- kspace_data: bfloat16 [32, 2, 128, 128, 128], P('coil', None, None, 'slab'), may hold values from -4 to 4
- coil_maps: bfloat16 [32, 2, 128, 128, 128], P('coil', None, 'slab'), may hold values from -1.796875 to 1.796875
- sample_mask: int32 [32, 128, 128], P('coil', None, 'slab'), may hold values 0 or 1
- initial_image: float32 [2, 128, 128, 128], P(None, 'slab', 'coil'), may hold values from -6 to 6
Outputs:
- image: float32 [2, 128, 128, 128], P(None, 'slab', 'coil')
All inputs are finite; a program needn't handle non-finite values. No bound on the sum of `sample_mask` on one device may be relied on, other than what follows from the above.
Results may differ from a plain program's by a relative error of at most 0.0045.
Values may be sent and summed in bfloat16 or wider, within the bound.
A program may use at most 128 MiB of HBM per device.

v0:
```python
import math
import jax
import jax.numpy as jnp
from jax import lax
from jax.sharding import PartitionSpec as P

NX = 128
NY = 128
NZ = 128
ITERS = 2
dual_step = 0.25
primal_step = 0.25
tv_weight = 0.5


def from_behind(block, axis, distance):
    devices = range(lax.axis_size(axis))
    route = [(i - distance, i) for i in devices if i - distance in devices]
    return lax.ppermute(block, axis, route)


def dft_table(length, inverse):
    counter = jnp.arange(length, dtype=jnp.int32)
    product = counter[:, None] * counter[None, :] % length
    phase = 2.0 * math.pi / length * product.astype(jnp.float32)
    scale = 1.0 / math.sqrt(length)
    real_part = jnp.cos(phase) * scale
    imag_part = jnp.sin(phase) * scale
    if not inverse:
        imag_part = -imag_part
    table = jnp.stack([jnp.stack([real_part, imag_part]), jnp.stack([-imag_part, real_part])])
    return table.astype(jnp.bfloat16)


def data_term(guess, coil_maps, kspace_data, sample_mask, dual_data, tables):
    forward_x, forward_y, forward_z, inverse_x, inverse_y, inverse_z = tables
    maps_real = coil_maps[:, 0].astype(jnp.float32)
    maps_imag = coil_maps[:, 1].astype(jnp.float32)
    pieces = jnp.stack(
        [maps_real * guess[0] - maps_imag * guess[1], maps_real * guess[1] + maps_imag * guess[0]],
        1,
    ).astype(jnp.bfloat16)
    pieces = jnp.einsum(
        "ckzyx,kjxw->cjzyw", pieces, forward_x, preferred_element_type=jnp.float32
    ).astype(jnp.bfloat16)
    pieces = jnp.einsum(
        "ckzyx,kjyv->cjzvx", pieces, forward_y, preferred_element_type=jnp.float32
    ).astype(jnp.bfloat16)
    spectrum = jnp.einsum(
        "ckzyx,kjzw->cjwyx",
        lax.all_to_all(pieces, "slab", split_axis=3, concat_axis=2, tiled=True),
        forward_z,
        preferred_element_type=jnp.float32,
    )
    sampled = sample_mask[:, None, :, :, None].astype(jnp.float32)
    dual_new = (
        dual_data + dual_step * (sampled * (spectrum - kspace_data.astype(jnp.float32)))
    ) / (1.0 + dual_step)
    back_field = jnp.einsum(
        "ckzyx,kjzw->cjwyx",
        dual_new.astype(jnp.bfloat16),
        inverse_z,
        preferred_element_type=jnp.float32,
    ).astype(jnp.bfloat16)
    back_field = jnp.einsum(
        "ckzyx,kjyv->cjzvx",
        lax.all_to_all(back_field, "slab", split_axis=2, concat_axis=3, tiled=True),
        inverse_y,
        preferred_element_type=jnp.float32,
    ).astype(jnp.bfloat16)
    back_field = jnp.einsum(
        "ckzyx,kjxw->cjzyw", back_field, inverse_x, preferred_element_type=jnp.float32
    )
    real_sum = jnp.sum(maps_real * back_field[:, 0] + maps_imag * back_field[:, 1], 0)
    imag_sum = jnp.sum(maps_real * back_field[:, 1] - maps_imag * back_field[:, 0], 0)
    return (jnp.stack([real_sum, imag_sum]), dual_new)


def tv_update(guess, duals):
    planes = guess.shape[1]
    plane_pos = lax.axis_index("slab") * planes + lax.broadcasted_iota(
        jnp.int32, (1, planes, 1, 1), 1
    )
    next_plane = from_behind(guess[:, :1], "slab", -1)
    ahead_z = jnp.concatenate([guess[:, 1:], next_plane], 1)
    grad_z = jnp.where(plane_pos < NZ - 1, ahead_z - guess, 0.0)
    grad_y = jnp.concatenate(
        [guess[:, :, 1:] - guess[:, :, :-1], jnp.zeros_like(guess[:, :, :1])], 2
    )
    grad_x = jnp.concatenate([guess[..., 1:] - guess[..., :-1], jnp.zeros_like(guess[..., :1])], 3)
    moved_z = duals[0] + dual_step * grad_z
    moved_y = duals[1] + dual_step * grad_y
    moved_x = duals[2] + dual_step * grad_x
    magnitude = jnp.sqrt(
        jnp.sum(moved_z * moved_z, 0)
        + jnp.sum(moved_y * moved_y, 0)
        + jnp.sum(moved_x * moved_x, 0)
    )
    factor = 1.0 / jnp.maximum(1.0, magnitude / tv_weight)
    dual_z = moved_z * factor
    dual_y = moved_y * factor
    dual_x = moved_x * factor
    prior_plane = from_behind(dual_z[:, -1:], "slab", 1)
    spread_z = jnp.concatenate([prior_plane, dual_z[:, :-1]], 1) - dual_z
    spread_y = jnp.concatenate([jnp.zeros_like(dual_y[:, :, :1]), dual_y[:, :, :-1]], 2) - dual_y
    spread_x = jnp.concatenate([jnp.zeros_like(dual_x[..., :1]), dual_x[..., :-1]], 3) - dual_x
    return ((dual_z, dual_y, dual_x), spread_z + spread_y + spread_x)


def on_device(kspace_data, coil_maps, sample_mask, initial_image):
    tables = (
        dft_table(NX, False),
        dft_table(NY, False),
        dft_table(NZ, False),
        dft_table(NX, True),
        dft_table(NY, True),
        dft_table(NZ, True),
    )
    dual_data = jnp.zeros(kspace_data.shape, jnp.float32)
    share_rows = initial_image.shape[2]
    current = initial_image
    guess = current
    duals = None
    for turn_index in range(ITERS):
        whole_guess = lax.all_gather(guess, "coil", axis=2, tiled=True)
        if duals is None:
            duals = (
                jnp.zeros_like(whole_guess),
                jnp.zeros_like(whole_guess),
                jnp.zeros_like(whole_guess),
            )
        data_grad, dual_data = data_term(
            whole_guess, coil_maps, kspace_data, sample_mask, dual_data, tables
        )
        data_grad = lax.psum_scatter(data_grad, "coil", scatter_dimension=2, tiled=True)
        duals, spread = tv_update(whole_guess, duals)
        spread_share = lax.dynamic_slice_in_dim(
            spread, lax.axis_index("coil") * share_rows, share_rows, 2
        )
        updated = current - primal_step * (data_grad + spread_share)
        guess = 2.0 * updated - current
        current = updated
    return current


def solution(mesh):
    placed = (
        P("coil", None, None, "slab", None),
        P("coil", None, "slab", None, None),
        P("coil", None, "slab"),
        P(None, "slab", "coil", None),
    )
    return jax.shard_map(
        on_device,
        mesh=mesh,
        in_specs=placed,
        out_specs=P(None, "slab", "coil", None),
        check_vma=False,
    )
```

profile of v0, /device:TPU:0, one launch (start us, length us, event | category | flops | bytes accessed | tf_op | source)
XLA Modules:
  0.0 1111.8 jit_solution(6184151116436738106)
XLA Ops:
  6.5 2.1 copy.138
  9.3 24.9 %all-gather.3.cloned.1.call-done = f32[2,16,128,128]{3,1,0,2:T(8,128)} async-done(((f32[2,16,32,128]{3,1,0,2:T(8,128)}), f32[2,16,128,128]{3,1,0,2:T(8,128)}) %all-gather.3.cloned.1.call-update) | async-done | bytes 2097168 | tf_op jit(solution)/shard_map/all_gather | solution.py:125
  34.2 1.9 slice_bitcast_fusion.3
  36.1 0.3 copy.119
  36.8 1.5 copy-done.1
  38.2 4.7 fusion.13
  43.0 9.0 fusion.8
  52.0 12.0 %copy.123 = bf16[8,2,16,128,128]{4,2,0,1,3:T(8,128)(2,1)} copy(bf16[8,2,16,128,128]{4,3,2,0,1:T(8,128)(2,1)} %fusion.8) | data formatting | bytes 16777216 | tf_op jit(solution)/shard_map/convert_element_type | solution.py:48
  64.0 5.6 all-to-all-start
  69.9 183.3 %all-to-all-done = bf16[8,2,16,128,128]{4,2,0,1,3:T(8,128)(2,1)} async-done(((bf16[8,2,16,128,128]{4,2,0,1,3:T(8,128)(2,1)}), bf16[8,2,16,128,128]{4,2,0,1,3:T(8,128)(2,1)}, u32[]{:S(2)}, u32[]{:S(2)}) %all-to-all-start) | async-done | bytes 8388640 | tf_op jit(solution)/shard_map/all_to_all | solution.py:51
  253.2 9.1 copy.124
  262.3 12.3 %fusion.7 = (bf16[8,2,128,16,128]{4,2,3,0,1:T(8,128)(2,1)S(1)}, f32[2,128,8,16,128,1]{4,1,5,3,2,0:T(8,128)}) fusion(f32[8,128,16]{1,2,0:T(8,128)S(1)} %convert_element_type.129, bf16[8,2,128,16,128]{4,3,2,1,0:T(8,128)(2,1)} %param.4, bf16[8,2,128,16,128,1]{4,2,1,3,0,5:T(8,128)(2,1)} %bitcast.269, bf16[1,2,128,128]{2,3,0,1:T(8,128)(2,1)S(1)} %get-tuple-element.28, ...), kind=kOutput, calls=%fused_computation.33 | convolution fusion | flops 2168717312 | bytes 42139648 | tf_op jit(solution)/shard_map/ckzyx,kjzw->cjwyx/dot_general | solution.py:49
  274.6 4.5 fusion.9
  279.1 12.0 %copy.128 = bf16[8,2,128,16,128]{4,3,0,1,2:T(8,128)(2,1)} copy(bf16[8,2,128,16,128]{4,2,3,0,1:T(8,128)(2,1)} %fusion.9) | data formatting | bytes 16777216 | tf_op jit(solution)/shard_map/convert_element_type | solution.py:64
  291.1 189.0 %all_to_all.72 = bf16[8,2,128,16,128]{4,3,0,1,2:T(8,128)(2,1)} all-to-all(bf16[8,2,128,16,128]{4,3,0,1,2:T(8,128)(2,1)} %copy.128), channel_id=1, replica_groups=mesh['coil'=4,'slab'=8] {'slab'}, dimensions={2} | all-to-all | bytes 16777216 | tf_op jit(solution)/shard_map/all_to_all | solution.py:67
  480.2 9.1 copy.130
  489.3 10.3 convolution_bitcast_fusion.1
  499.5 10.0 fusion.17
  510.2 1.4 pad_maximum_fusion
  511.6 3.3 copy.137
  515.2 1.3 collective-permute-start
  516.5 0.6 slice_subtract_fusion.1
  517.5 0.7 multiply_reduce_fusion.3
  518.3 3.8 collective-permute-done
  522.0 0.8 multiply_reduce_fusion.5
  522.8 0.5 divide_multiply_fusion
  523.3 3.2 broadcast_multiply_fusion.3
  526.5 1.3 copy-done.6
  528.0 4.5 collective-permute-start.1
  532.5 3.1 slice.142
  535.5 8.4 reduce-scatter.3.cloned.1.call-done
  544.0 3.2 multiply_subtract_fusion
  547.2 22.7 %all-gather.5.cloned.1.call-done = f32[2,16,128,128]{3,1,0,2:T(8,128)} async-done(((f32[2,16,32,128]{3,1,0,2:T(8,128)}), f32[2,16,128,128]{3,1,0,2:T(8,128)}) %all-gather.5.cloned.1.call-update) | async-done | bytes 2097168 | tf_op jit(solution)/shard_map/all_gather | solution.py:125
  569.9 1.7 slice_bitcast_fusion.1
  572.3 8.2 fusion.21
  580.5 9.0 fusion.10
  589.5 12.0 %copy.143 = bf16[8,2,16,128,128]{4,2,0,1,3:T(8,128)(2,1)} copy(bf16[8,2,16,128,128]{4,3,2,0,1:T(8,128)(2,1)} %fusion.10) | data formatting | bytes 16777216 | tf_op jit(solution)/shard_map/convert_element_type | solution.py:48
  601.5 189.6 %all_to_all.73 = bf16[8,2,16,128,128]{4,2,0,1,3:T(8,128)(2,1)} all-to-all(bf16[8,2,16,128,128]{4,2,0,1,3:T(8,128)(2,1)} %copy.143), channel_id=1, replica_groups=mesh['coil'=4,'slab'=8] {'slab'}, dimensions={3} | all-to-all | bytes 16777216 | tf_op jit(solution)/shard_map/all_to_all | solution.py:51
  791.0 16.3 %copy.145 = bf16[8,2,8,16,16,128]{5,4,3,2,1,0:T(8,128)(2,1)} copy(bf16[8,2,8,16,16,128]{5,3,0,1,4,2:T(8,128)(2,1)} %bitcast.273) | data formatting | bytes 16777216 | tf_op jit(solution)/shard_map/all_to_all | solution.py:51
  807.3 21.2 %fusion.6 = bf16[8,2,128,16,128]{4,2,3,0,1:T(8,128)(2,1)} fusion(f32[2,128,8,16,128,1]{4,1,5,3,2,0:T(8,128)} %get-tuple-element.34, f32[8,128,16]{1,2,0:T(8,128)S(1)} %convert_element_type.129, bf16[8,2,128,16,128]{4,3,2,1,0:T(8,128)(2,1)} %param.4, bf16[8,2,128,16,128]{4,3,2,1,0:T(8,128)(2,1)} %bitcast.278, ...), kind=kOutput, calls=%fused_computation.24 | convolution fusion | flops 2189688832 | bytes 42139648 | tf_op jit(solution)/shard_map/ckzyx,kjzw->cjwyx/dot_general | solution.py:49
  828.5 8.0 fusion.11
  836.5 12.0 %copy.149 = bf16[8,2,128,16,128]{4,3,0,1,2:T(8,128)(2,1)} copy(bf16[8,2,128,16,128]{4,2,3,0,1:T(8,128)(2,1)} %fusion.11) | data formatting | bytes 16777216 | tf_op jit(solution)/shard_map/convert_element_type | solution.py:64
  848.5 188.8 %all_to_all.74 = bf16[8,2,128,16,128]{4,3,0,1,2:T(8,128)(2,1)} all-to-all(bf16[8,2,128,16,128]{4,3,0,1,2:T(8,128)(2,1)} %copy.149), channel_id=1, replica_groups=mesh['coil'=4,'slab'=8] {'slab'}, dimensions={2} | all-to-all | bytes 16777216 | tf_op jit(solution)/shard_map/all_to_all | solution.py:67
  1037.3 9.1 copy.151
  1046.4 10.3 convolution_bitcast_fusion
  1056.7 10.0 fusion.25
  1067.4 1.4 pad_maximum_fusion.1
  1068.8 3.3 copy.158
  1072.3 1.6 collective-permute-start.2
  1074.1 0.6 slice_subtract_fusion
  1074.7 1.0 copy-done.4
  1075.7 0.6 multiply_reduce_fusion
  1076.6 1.6 copy-done.5
  1078.1 0.6 multiply_reduce_fusion.1
  1078.7 0.4 collective-permute-done.2
  1079.1 1.0 multiply_reduce_fusion.2
  1080.1 0.4 maximum_divide_fusion
  1080.5 2.7 broadcast_multiply_fusion.2
  1083.4 4.7 collective-permute-start.3
  1088.1 1.5 slice.156
  1089.7 1.0 collective-permute-done.3
  1090.6 10.9 reduce-scatter.5.cloned.1.call-done
  1101.5 2.1 fusion.85
  1103.7 1.1 copy.159
  (49 shorter events, 4.7 us)
Async XLA Ops:
  6.5 27.7 %all-gather.3.cloned.1.call-start = ((), (), s32[]{:S(2)}) async-start(), calls=%async_computation.6 | async-start | bytes 2621440 | tf_op jit(solution)/shard_map/all_gather | solution.py:125
  34.2 4.0 copy-start.1
  64.0 5.9 copy-start.11
  64.0 189.2 %all-to-all-start = ((bf16[8,2,16,128,128]{4,2,0,1,3:T(8,128)(2,1)}), bf16[8,2,16,128,128]{4,2,0,1,3:T(8,128)(2,1)}, u32[]{:S(2)}, u32[]{:S(2)}) async-start(bf16[8,2,16,128,128]{4,2,0,1,3:T(8,128)(2,1)} %copy.123), calls=%async_computation | async-start | bytes 16777216 | tf_op jit(solution)/shard_map/all_to_all | solution.py:51
  69.6 474.3 %reduce-scatter.3.cloned.1.call-start = ((), (), s32[]{:S(2)}) async-start(), calls=%async_computation.7 | async-start | bytes 2621440 | tf_op jit(solution)/shard_map/reduce_scatter | solution.py:135
  511.6 3.4 copy-start
  515.0 54.9 %all-gather.5.cloned.1.call-start = ((), (), s32[]{:S(2)}) async-start(), calls=%async_computation.8 | async-start | bytes 2621440 | tf_op jit(solution)/shard_map/all_gather | solution.py:125
  515.2 6.9 collective-permute-start
  526.5 1.3 copy-start.6
  526.5 17.4 %copy-start.3 = (f32[2,16,128,128]{3,1,0,2:T(8,128)S(1)}, f32[2,16,128,128]{3,1,0,2:T(8,128)}, u32[]{:S(2)}) copy-start(f32[2,16,128,128]{3,1,0,2:T(8,128)} %get-tuple-element.26) | copy-start | bytes 6291460
  526.5 17.4 %copy-start.10 = (f32[2,16,32,128]{3,2,1,0:T(8,128)S(1)}, f32[2,16,32,128]{3,2,1,0:T(8,128)}, u32[]{:S(2)}) copy-start(f32[2,16,32,128]{3,2,1,0:T(8,128)} %param.7) | copy-start | bytes 1572868
  528.0 7.5 collective-permute-start.1
  547.2 554.4 %reduce-scatter.5.cloned.1.call-start = ((), (), s32[]{:S(2)}) async-start(), calls=%async_computation.9 | async-start | bytes 2621440 | tf_op jit(solution)/shard_map/reduce_scatter | solution.py:135
  1068.8 3.3 copy-start.2
  1072.3 6.9 collective-permute-start.2
  1074.1 1.6 copy-start.4
  1076.3 1.8 copy-start.5
  1076.3 2.8 copy-start.7
  1083.3 4.9 copy-start.8
  1083.3 18.3 %copy-start.9 = (f32[2,16,32,128]{3,1,0,2:T(8,128)S(1)}, f32[2,16,32,128]{3,1,0,2:T(8,128)}, u32[]{:S(2)}) copy-start(f32[2,16,32,128]{3,1,0,2:T(8,128)} %get-tuple-element.12) | copy-start | bytes 1572868
  1083.4 7.2 collective-permute-start.3
Sparse Core Ops, SparseCore 0:
  8.9 25.2 all-gather.2
  515.1 28.8 reduce-scatter.2
  547.3 22.5 all-gather.4
  1072.3 29.2 reduce-scatter.4
where the time goes:
time: 1120 us; the launch traced here: 1110 us
  blocking collectives  567 us (51%)
  waiting for transfers between devices  255 us (23%)
  local copies, waits for them, and re-layouts  119 us (11%)
  matrix products  84.5 us (8%)
  other arithmetic  53.8 us (5%)
  starting transfers between devices  18 us (2%)
  between operations  14 us (1%)
    all_to_all x2, blocking collectives, data_term(): lax.all_to_all(back_field, 'slab', split_axis=2, concat_axis=3, tiled=True)  378 us
    all_to_all x1, blocking collectives, data_term(): lax.all_to_all(pieces, 'slab', split_axis=3, concat_axis=2, tiled=True)  190 us
    all_to_all x1, waiting for transfers between devices, data_term(): lax.all_to_all(pieces, 'slab', split_axis=3, concat_axis=2, tiled=True)  183 us
    all_gather x2, waiting for transfers between devices, on_device(): whole_guess = lax.all_gather(guess, 'coil', axis=2, tiled=True)  47.6 us
    dot_general x2, matrix products, data_term(): jnp.einsum('ckzyx,kjzw->cjwyx', lax.all_to_all(pieces, 'slab', split_axis...  33.5 us
    all_to_all x2, local copies, waits for them, and re-layouts, data_term(): lax.all_to_all(pieces, 'slab', split_axis=3, concat_axis=2, tiled=True)  25.4 us
    convert_element_type x2, local copies, waits for them, and re-layouts, data_term(): back_field = jnp.einsum('ckzyx,kjzw->cjwyx', dual_new.astype(jnp.bfloat16...  24 us
    convert_element_type x2, local copies, waits for them, and re-layouts, data_term(): pieces = jnp.einsum('ckzyx,kjyv->cjzvx', pieces, forward_y, preferred_ele...  24 us
  transfers between devices with their start and end apart: 9, of which 8 were waited for; matrix products, arithmetic and copies ran while one was open for 2% of the time, Pallas kernels for 0%

commit v1 on v0

--- a/solution.py
+++ b/solution.py
@@ -48,7 +48,12 @@
     ).astype(jnp.bfloat16)
     spectrum = jnp.einsum(
         "ckzyx,kjzw->cjwyx",
-        lax.all_to_all(pieces, "slab", split_axis=3, concat_axis=2, tiled=True),
+        jnp.concatenate(
+            lax.all_to_all(
+                jnp.stack(jnp.split(pieces, lax.axis_size("slab"), axis=3)), "slab", 0, 0
+            ),
+            axis=2,
+        ),
         forward_z,
         preferred_element_type=jnp.float32,
     )

time: 1120 us -> 1140 us (1.018)
    unnamed x29 -> x41, local copies, waits for them, and re-layouts: 8.87 us -> 42.1 us
    all_to_all x2 -> x0, local copies, waits for them, and re-layouts: 25.4 us -> none  [data_term(): lax.all_to_all(pieces, 'slab', split_axis=3, concat_axis=2, tiled=True)]
    convert_element_type x2 -> x0, local copies, waits for them, and re-layouts: 24 us -> none  [data_term(): pieces = jnp.einsum('ckzyx,kjyv->cjzvx', pieces, forward_y, preferred_ele...]
    reshape x0 -> x2, local copies, waits for them, and re-layouts: none -> 19.5 us  [data_term(): jnp.concatenate(lax.all_to_all(jnp.stack(jnp.split(pieces, lax.axis_size(...]
  transfers between devices with their start and end apart: 9 -> 9, of which waited for: 8 -> 9; matrix products, arithmetic and copies ran while one was open for 2% -> 2% of each run, Pallas kernels for 0% -> 0%
where the time goes in v1:
time: 1140 us; the launch traced here: 1130 us
  blocking collectives  567 us (50%)
  waiting for transfers between devices  259 us (23%)
  local copies, waits for them, and re-layouts  124 us (11%)
  matrix products  91.8 us (8%)
  other arithmetic  59.3 us (5%)
  starting transfers between devices  17.3 us (2%)
  between operations  14 us (1%)
    all_to_all x2, blocking collectives, data_term(): lax.all_to_all(back_field, 'slab', split_axis=2, concat_axis=3, tiled=True)  378 us
    all_to_all x1, blocking collectives, data_term(): lax.all_to_all(jnp.stack(jnp.split(pieces, lax.axis_size('slab'), axis=3)...  189 us
    all_to_all x1, waiting for transfers between devices, data_term(): lax.all_to_all(jnp.stack(jnp.split(pieces, lax.axis_size('slab'), axis=3)...  183 us
    all_gather x2, waiting for transfers between devices, on_device(): whole_guess = lax.all_gather(guess, 'coil', axis=2, tiled=True)  47.6 us
    unnamed x41, local copies, waits for them, and re-layouts  42.1 us
    dot_general x2, matrix products, data_term(): jnp.einsum('ckzyx,kjzw->cjwyx', jnp.concatenate(lax.all_to_all(jnp.stack(...  37.2 us
    convert_element_type x2, local copies, waits for them, and re-layouts, data_term(): back_field = jnp.einsum('ckzyx,kjzw->cjwyx', dual_new.astype(jnp.bfloat16...  24 us
  transfers between devices with their start and end apart: 9, of which 9 were waited for; matrix products, arithmetic and copies ran while one was open for 2% of the time, Pallas kernels for 0%

profile of v1, /device:TPU:0, one launch (start us, length us, event | category | flops | bytes accessed | tf_op | source)
XLA Modules:
  0.0 1132.6 jit_solution(1329772320350368935)
XLA Ops:
  6.5 2.1 copy.136
  9.3 24.9 %all-gather.3.cloned.1.call-done = f32[2,16,128,128]{3,1,0,2:T(8,128)} async-done(((f32[2,16,32,128]{3,1,0,2:T(8,128)}), f32[2,16,128,128]{3,1,0,2:T(8,128)}) %all-gather.3.cloned.1.call-update) | async-done | bytes 2097168 | tf_op jit(solution)/shard_map/all_gather | solution.py:130
  34.2 1.9 slice_bitcast_fusion.19
  38.2 4.7 fusion.13
  42.9 9.0 fusion.8
  51.9 2.5 fusion.91
  54.5 2.4 fusion.90
  56.9 2.5 fusion.89
  59.4 2.5 fusion.88
  61.9 2.5 fusion.87
  64.4 2.5 fusion.86
  66.9 2.5 fusion.85
  69.3 2.5 fusion.84
  71.8 5.6 all-to-all-start
  77.5 183.5 %all-to-all-done = bf16[8,8,2,16,16,128]{5,4,3,1,2,0:T(8,128)(2,1)} async-done(((bf16[8,8,2,16,16,128]{5,4,3,1,2,0:T(8,128)(2,1)}), bf16[8,8,2,16,16,128]{5,4,3,1,2,0:T(8,128)(2,1)}, u32[]{:S(2)}, u32[]{:S(2)}) %all-to-all-start) | async-done | bytes 8388640 | tf_op jit(solution)/shard_map/all_to_all | solution.py:52
  261.0 9.8 copy.121
  270.8 16.2 %fusion.7 = (bf16[8,2,128,16,128]{4,2,3,0,1:T(8,128)(2,1)}, f32[2,128,8,16,128,1]{4,1,5,3,2,0:T(8,128)}) fusion(f32[8,128,16]{1,2,0:T(8,128)S(1)} %convert_element_type.129, bf16[8,2,128,16,128]{4,3,2,1,0:T(8,128)(2,1)} %param.4, bf16[8,2,128,16,128]{4,3,2,1,0:T(8,128)(2,1)} %bitcast.331, bf16[1,2,128,128]{2,3,0,1:T(8,128)(2,1)S(1)} %get-tuple-element.28, ...), kind=kOutput, calls=%fused_computation.33 | convolution fusion | flops 2168717312 | bytes 42139648 | tf_op jit(solution)/shard_map/ckzyx,kjzw->cjwyx/dot_general | solution.py:49
  287.0 8.0 fusion.9
  295.0 12.0 %copy.126 = bf16[8,2,128,16,128]{4,3,0,1,2:T(8,128)(2,1)} copy(bf16[8,2,128,16,128]{4,2,3,0,1:T(8,128)(2,1)} %fusion.9) | data formatting | bytes 16777216 | tf_op jit(solution)/shard_map/convert_element_type | solution.py:69
  307.0 189.2 %all_to_all.46 = bf16[8,2,128,16,128]{4,3,0,1,2:T(8,128)(2,1)} all-to-all(bf16[8,2,128,16,128]{4,3,0,1,2:T(8,128)(2,1)} %copy.126), channel_id=1, replica_groups=mesh['coil'=4,'slab'=8] {'slab'}, dimensions={2} | all-to-all | bytes 16777216 | tf_op jit(solution)/shard_map/all_to_all | solution.py:72
  496.2 9.1 copy.128
  505.3 10.3 convolution_bitcast_fusion.1
  515.6 11.3 fusion.17
  526.9 1.7 copy.207
  528.6 2.6 copy.206
  531.2 2.8 pad_maximum_fusion
  533.9 3.1 copy.135
  540.3 3.8 collective-permute-done
  545.4 3.3 broadcast_multiply_fusion.3
  550.2 4.1 collective-permute-start.1
  554.3 1.8 slice.142
  556.6 9.4 reduce-scatter.3.cloned.1.call-done
  566.0 3.4 multiply_subtract_fusion
  569.5 22.7 %all-gather.5.cloned.1.call-done = f32[2,16,128,128]{3,1,0,2:T(8,128)} async-done(((f32[2,16,32,128]{3,1,0,2:T(8,128)}), f32[2,16,128,128]{3,1,0,2:T(8,128)}) %all-gather.5.cloned.1.call-update) | async-done | bytes 2097168 | tf_op jit(solution)/shard_map/all_gather | solution.py:130
  592.1 1.7 slice_bitcast_fusion.9
  594.5 8.1 fusion.21
  602.6 9.0 fusion.10
  613.1 1.6 fusion.82
  614.6 1.6 fusion.81
  616.2 1.6 fusion.80
  617.8 1.6 fusion.79
  619.3 1.6 fusion.78
  620.9 1.6 fusion.77
  622.5 1.6 fusion.76
  624.0 189.0 %all_to_all.47 = bf16[8,8,2,16,16,128]{5,4,3,1,2,0:T(8,128)(2,1)} all-to-all(bf16[8,8,2,16,16,128]{5,4,3,1,2,0:T(8,128)(2,1)S(1)} %fusion.76), channel_id=1, replica_groups=mesh['coil'=4,'slab'=8] {'slab'}, dimensions={0} | all-to-all | bytes 16777216 | tf_op jit(solution)/shard_map/all_to_all | solution.py:52
  813.1 9.8 copy.141
  822.8 21.0 %fusion.6 = bf16[8,2,128,16,128]{4,2,3,0,1:T(8,128)(2,1)} fusion(f32[2,128,8,16,128,1]{4,1,5,3,2,0:T(8,128)} %get-tuple-element.34, f32[8,128,16]{1,2,0:T(8,128)S(1)} %convert_element_type.129, bf16[8,2,128,16,128]{4,3,2,1,0:T(8,128)(2,1)} %param.4, bf16[8,2,128,16,128]{4,3,2,1,0:T(8,128)(2,1)} %bitcast.340, ...), kind=kOutput, calls=%fused_computation.24 | convolution fusion | flops 2189688832 | bytes 42139648 | tf_op jit(solution)/shard_map/ckzyx,kjzw->cjwyx/dot_general | solution.py:49
  843.8 8.0 fusion.11
  851.8 12.0 %copy.145 = bf16[8,2,128,16,128]{4,3,0,1,2:T(8,128)(2,1)} copy(bf16[8,2,128,16,128]{4,2,3,0,1:T(8,128)(2,1)} %fusion.11) | data formatting | bytes 16777216 | tf_op jit(solution)/shard_map/convert_element_type | solution.py:69
  863.8 188.7 %all_to_all.48 = bf16[8,2,128,16,128]{4,3,0,1,2:T(8,128)(2,1)} all-to-all(bf16[8,2,128,16,128]{4,3,0,1,2:T(8,128)(2,1)} %copy.145), channel_id=1, replica_groups=mesh['coil'=4,'slab'=8] {'slab'}, dimensions={2} | all-to-all | bytes 16777216 | tf_op jit(solution)/shard_map/all_to_all | solution.py:72
  1052.5 9.1 copy.147
  1061.7 10.3 convolution_bitcast_fusion
  1071.9 11.3 fusion.25
  1083.3 1.7 copy.209
  1085.0 2.5 copy.208
  1087.5 2.7 pad_maximum_fusion.1
  1090.2 3.1 copy.154
  1093.5 1.7 collective-permute-start.2
  1098.0 2.5 collective-permute-done.2
  1101.9 2.8 broadcast_multiply_fusion.2
  1104.8 4.4 collective-permute-start.3
  1109.3 1.5 slice.156
  1111.8 10.5 reduce-scatter.5.cloned.1.call-done
  1122.3 2.1 fusion.104
  (61 shorter events, 17.9 us)
Async XLA Ops:
  6.5 27.7 %all-gather.3.cloned.1.call-start = ((), (), s32[]{:S(2)}) async-start(), calls=%async_computation.6 | async-start | bytes 2621440 | tf_op jit(solution)/shard_map/all_gather | solution.py:130
  34.2 4.0 copy-start.1
  71.8 5.7 copy-start.10
  71.8 189.2 %all-to-all-start = ((bf16[8,8,2,16,16,128]{5,4,3,1,2,0:T(8,128)(2,1)}), bf16[8,8,2,16,16,128]{5,4,3,1,2,0:T(8,128)(2,1)}, u32[]{:S(2)}, u32[]{:S(2)}) async-start(bf16[8,8,2,16,16,128]{5,4,3,1,2,0:T(8,128)(2,1)} %fusion.84), calls=%async_computation | async-start | bytes 16777216 | tf_op jit(solution)/shard_map/all_to_all | solution.py:52
  77.5 488.6 %reduce-scatter.3.cloned.1.call-start = ((), (), s32[]{:S(2)}) async-start(), calls=%async_computation.7 | async-start | bytes 2621440 | tf_op jit(solution)/shard_map/reduce_scatter | solution.py:140
  526.9 10.2 copy-start
  537.1 55.1 %all-gather.5.cloned.1.call-start = ((), (), s32[]{:S(2)}) async-start(), calls=%async_computation.8 | async-start | bytes 2621440 | tf_op jit(solution)/shard_map/all_gather | solution.py:130
  537.2 6.9 collective-permute-start
  545.4 20.7 %copy-start.9 = (f32[2,16,32,128]{3,2,1,0:T(8,128)S(1)}, f32[2,16,32,128]{3,2,1,0:T(8,128)}, u32[]{:S(2)}) copy-start(f32[2,16,32,128]{3,2,1,0:T(8,128)} %param.7) | copy-start | bytes 1572868
  548.7 1.3 copy-start.5
  550.2 6.4 collective-permute-start.1
  569.4 552.9 %reduce-scatter.5.cloned.1.call-start = ((), (), s32[]{:S(2)}) async-start(), calls=%async_computation.9 | async-start | bytes 2621440 | tf_op jit(solution)/shard_map/reduce_scatter | solution.py:140
  1083.2 10.1 copy-start.2
  1093.4 2.7 copy-start.3
  1093.5 7.0 collective-permute-start.2
  1095.5 1.9 copy-start.4
  1096.1 4.4 copy-start.6
  1101.9 20.4 %copy-start.8 = (f32[2,16,32,128]{3,1,0,2:T(8,128)S(1)}, f32[2,16,32,128]{3,1,0,2:T(8,128)}, u32[]{:S(2)}) copy-start(f32[2,16,32,128]{3,1,0,2:T(8,128)} %get-tuple-element.12) | copy-start | bytes 1572868
  1104.7 4.6 copy-start.7
  1104.8 6.9 collective-permute-start.3
Sparse Core Ops, SparseCore 0:
  8.9 25.2 all-gather.2
  537.2 28.8 reduce-scatter.2
  569.5 22.5 all-gather.4
  1093.5 28.7 reduce-scatter.4
